TPU v7x, 32 devices: a whole 2x2x4 slice. The times are simulated.
32 devices in a mesh: pts: 4 (over y, core), dir: 4 (over z), freq: 2 (over x).
Axes of the slice: x: 2, y: 2, z: 4, core: 2. Of those that a mesh axis runs over, the one named last changes fastest.
Arguments:
- action: float32 [48, 64, 16384], P('freq', 'dir', 'pts'), may hold values from 0.05 to 2
- bathymetry: float32 [16384], P('pts'), may hold values from 20 to 60
- refraction: float32 [48, 16384], P('freq', 'pts'), may hold values from 0.5 to 2
- shifting: float32 [48, 16384], P('freq', 'pts'), may hold values from 0.5 to 2
- heading: float32 [16384], P('pts'), may hold values from -3.140625 to 3.140625
- slope_angle: float32 [16384], P('pts'), may hold values from -3.140625 to 3.140625
- wet_mask: int32 [16384], P('pts'), may hold values 0 or 1
- substeps: int32 [32], P('pts'), may hold values from 1 to 4
Outputs:
- evolved: float32 [48, 64, 16384], P('freq', 'dir', 'pts')
All inputs are finite; a program needn't handle non-finite values. Where the computation divides by a largest or mean magnitude, that divisor is 1e-20 or more. No bound on the sum of `wet_mask` on one device may be relied on, other than what follows from the above.
Results may differ from a plain program's by a relative error of at most 0.00002.
Values sent between devices are 32-bit elements; how exact they have to be, the bound alone decides.
A program may use at most 64 MiB of HBM per device.

v0:
```python
import functools
import math

import jax
import jax.numpy as jnp
from jax import lax
from jax.experimental import pallas as pl
from jax.experimental.pallas import tpu as pltpu
from jax.sharding import PartitionSpec as P

FREQ = 48
DIR = 64
KMAX = 4
BLK = 512
CHUNK = 256
HALO = KMAX
SUB = 8

EPSILON = 1e-06
MESH = pl.DeviceIdType.MESH


def kernel(
    n_pts,
    n_dir,
    n_freq,
    action_ref,
    depth_ref,
    refraction_ref,
    shifting_ref,
    heading_ref,
    slope_ref,
    wet_ref,
    substeps_ref,
    out_ref,
    own,
    upper,
    lower,
    ext,
    shext,
    face_shift,
    turn_row,
    shift_row,
    count_row,
    trig,
    depth_in,
    peaks,
    own_sem,
    dir_send,
    dir_recv,
    freq_send,
    freq_recv,
    sh_send,
    sh_recv,
    depth_send,
    depth_recv,
    peak_send,
    peak_recv,
):
    freq_local, dir_local, points = own.shape
    chunks = points // CHUNK
    rows = -(-(dir_local + 2 * HALO) // SUB) * SUB
    pts_at = lax.axis_index("pts")
    dir_at = lax.axis_index("dir")
    freq_at = lax.axis_index("freq")
    dir_up, dir_down = lax.rem(dir_at + 1, n_dir), lax.rem(dir_at + n_dir - 1, n_dir)
    pts_up, pts_down = lax.rem(pts_at + 1, n_pts), lax.rem(pts_at + n_pts - 1, n_pts)
    group = n_pts * n_freq
    member = pts_at * n_freq + freq_at
    has_above = freq_at < n_freq - 1
    has_below = freq_at > 0

    def peer(offset):
        other = lax.rem(member + offset, group)
        return {"pts": other // n_freq, "freq": lax.rem(other, n_freq)}

    barrier = pltpu.get_barrier_semaphore()
    for target in (dir_up, dir_down):
        pl.semaphore_signal(barrier, inc=1, device_id={"dir": target}, device_id_type=MESH)
    for offset in range(1, group):
        pl.semaphore_signal(barrier, inc=1, device_id=peer(offset), device_id_type=MESH)
    pl.semaphore_wait(barrier, 2 + group - 1)

    def span(c):
        return pl.ds(pl.multiple_of(c * CHUNK, CHUNK), CHUNK)

    def remote(src, dst, send, recv, where):
        return pltpu.make_async_remote_copy(
            src_ref=src, dst_ref=dst, send_sem=send, recv_sem=recv, device_id=where, device_id_type=MESH
        )

    def depth_copies():
        return (
            remote(
                depth_ref.at[:, pl.ds(points - 128, 128)],
                depth_in.at[0],
                depth_send.at[0],
                depth_recv.at[0],
                {"pts": pts_up},
            ),
            remote(
                depth_ref.at[:, pl.ds(0, 128)],
                depth_in.at[1],
                depth_send.at[1],
                depth_recv.at[1],
                {"pts": pts_down},
            ),
        )

    def dir_copies(c):
        return (
            remote(
                action_ref.at[:, pl.ds(dir_local - HALO, HALO), span(c)],
                lower.at[:, :, span(c)],
                dir_send.at[0, c],
                dir_recv.at[0, c],
                {"dir": dir_up},
            ),
            remote(
                action_ref.at[:, pl.ds(0, HALO), span(c)],
                upper.at[:, :, span(c)],
                dir_send.at[1, c],
                dir_recv.at[1, c],
                {"dir": dir_down},
            ),
        )

    def own_copy(c):
        return pltpu.make_async_copy(action_ref.at[:, :, span(c)], own.at[:, :, span(c)], own_sem.at[c])

    above, below = lax.rem(freq_at + 1, n_freq), lax.rem(freq_at + n_freq - 1, n_freq)

    def rise(src, dst, send, recv):
        return remote(src, dst, send, recv, {"freq": above})

    def fall(src, dst, send, recv):
        return remote(src, dst, send, recv, {"freq": below})

    def freq_copies(c):
        return (
            rise(
                ext.at[pl.ds(freq_local, HALO), :, span(c)],
                ext.at[pl.ds(0, HALO), :, span(c)],
                freq_send.at[0, c],
                freq_recv.at[0, c],
            ),
            fall(
                ext.at[pl.ds(HALO, HALO), :, span(c)],
                ext.at[pl.ds(freq_local + HALO, HALO), :, span(c)],
                freq_send.at[1, c],
                freq_recv.at[1, c],
            ),
        )

    def sh_copies():
        return (
            rise(
                shifting_ref.at[pl.ds(freq_local - SUB, SUB)],
                shext.at[0],
                sh_send.at[0],
                sh_recv.at[0],
            ),
            fall(shifting_ref.at[pl.ds(0, SUB)], shext.at[1], sh_send.at[1], sh_recv.at[1]),
        )

    def start_pair(pair):
        @pl.when(has_above)
        def _():
            pair[0].start()

        @pl.when(has_below)
        def _():
            pair[1].start()

    def wait_pair(pair):
        @pl.when(has_above)
        def _():
            pair[0].wait_send()
            pair[1].wait_recv()

        @pl.when(has_below)
        def _():
            pair[1].wait_send()
            pair[0].wait_recv()

    for copy in depth_copies():
        copy.start()

    @pl.loop(0, chunks)
    def _(c):
        for copy in dir_copies(c):
            copy.start()
        own_copy(c).start()

    start_pair(sh_copies())

    row = lax.broadcasted_iota(jnp.int32, (rows, CHUNK), 0)
    offset = jnp.where(row >= rows - HALO, row - rows, row)
    angle = ((dir_at * dir_local + offset).astype(jnp.float32) + 0.5) * (2.0 * math.pi / DIR)
    trig[0] = jnp.sin(angle)
    trig[1] = jnp.cos(angle)
    half = lax.broadcasted_iota(jnp.int32, (DIR // 2, 128), 0)
    half_angle = (half.astype(jnp.float32) + 0.5) * (2.0 * math.pi / DIR)
    half_sin, half_cos = jnp.sin(half_angle), jnp.cos(half_angle)
    wet = wet_ref[...].astype(jnp.float32)
    trig_row = (jnp.sin(slope_ref[...]), jnp.cos(slope_ref[...]), jnp.sin(heading_ref[...]), jnp.cos(heading_ref[...]))
    turn_row[1:2, :] = trig_row[0]
    turn_row[2:3, :] = trig_row[1]
    shift_row[1:2, :] = trig_row[2]
    shift_row[2:3, :] = trig_row[3]

    @pl.when(jnp.logical_not(has_below))
    def _():
        @pl.loop(0, HALO)
        def _(f):
            ext[f] = jnp.zeros((dir_local, points), jnp.float32)

    @pl.when(jnp.logical_not(has_above))
    def _():
        @pl.loop(freq_local + HALO, freq_local + 2 * HALO)
        def _(f):
            ext[f] = jnp.zeros((dir_local, points), jnp.float32)

    for copy in depth_copies():
        copy.wait()
    depth = depth_ref[...]
    lane = lax.broadcasted_iota(jnp.int32, (1, points), 1)
    before = jnp.where(pts_at == 0, depth[:, :1], depth_in[0][:, 127:128])
    after = jnp.where(pts_at == n_pts - 1, depth[:, points - 1 :], depth_in[1][:, :1])
    left = jnp.where(lane == 0, before, pltpu.roll(depth, 1, 1))
    right = jnp.where(lane == points - 1, after, pltpu.roll(depth, points - 1, 1))
    slope = (right - left) * 0.5 * wet
    turn_row[0:1, :] = slope
    shift_row[0:1, :] = wet

    def peak_step(i, carry):
        turn, shift = carry
        part = pl.ds(pl.multiple_of(i * 128, 128), 128)
        sines = jnp.abs(half_sin * turn_row[2:3, part] - half_cos * turn_row[1:2, part])
        cosines = jnp.abs(half_cos * shift_row[2:3, part] + half_sin * shift_row[1:2, part])
        turn_peak = jnp.max(sines, axis=0, keepdims=True) * jnp.abs(turn_row[0:1, part])
        shift_peak = jnp.max(cosines, axis=0, keepdims=True) * shift_row[0:1, part]
        turn = jnp.maximum(turn, jnp.abs(refraction_ref[:, part]) * turn_peak)
        shift = jnp.maximum(shift, jnp.abs(shifting_ref[:, part]) * shift_peak)
        return turn, shift

    zero = jnp.zeros((freq_local, 128), jnp.float32)
    turn, shift = lax.fori_loop(0, points // 128, peak_step, (zero, zero))
    turn = jnp.max(jnp.max(turn, axis=0, keepdims=True), axis=1, keepdims=True)
    shift = jnp.max(jnp.max(shift, axis=0, keepdims=True), axis=1, keepdims=True)
    tile = lax.broadcasted_iota(jnp.int32, (SUB, 128), 0)
    peaks[member] = jnp.where(tile < SUB // 2, turn, shift)

    wait_pair(sh_copies())
    face_rows = freq_local + 2 * HALO
    first = freq_at * freq_local - HALO

    @pl.loop(0, points // CHUNK)
    def _(c):
        part = span(c)
        window = jnp.concatenate(
            [shext[0, :, part][SUB - HALO :], shifting_ref[:, part], shext[1, :, part][:HALO]], axis=0
        )
        following = jnp.concatenate([window[1:], window[:1]], axis=0)
        mark = first + lax.broadcasted_iota(jnp.int32, (face_rows, CHUNK), 0)
        valid = (mark >= 0) & (mark + 1 <= FREQ - 1)
        face_shift[:, part] = jnp.where(valid, 0.5 * (window + following), 0.0)

    def peak_copy(offset):
        return remote(
            peaks.at[member], peaks.at[member], peak_send.at[offset], peak_recv.at[offset], peer(offset)
        )

    def peak_arrival(offset):
        source = lax.rem(member + group - offset, group)
        return remote(
            peaks.at[source], peaks.at[source], peak_send.at[offset], peak_recv.at[offset], peer(offset)
        )

    for offset in range(1, group):
        peak_copy(offset).start()
    for offset in range(1, group):
        peak_copy(offset).wait_send()
        peak_arrival(offset).wait_recv()
    top = jnp.max(peaks[...], axis=0)
    scale_turn = 0.5 / (top[0:1, 0:1] + EPSILON)
    scale_shift = 0.5 / (top[SUB // 2 : SUB // 2 + 1, 0:1] + EPSILON)
    for block in range(points // BLK):
        part = pl.ds(block * BLK, BLK)
        count_row[0:1, part] = jnp.broadcast_to(
            substeps_ref[0:1, block : block + 1].astype(jnp.float32), (1, BLK)
        )
    count = count_row[0:1, :]
    turn_row[0:1, :] = turn_row[0:1, :] * scale_turn / count
    shift_row[3:4, :] = shift_row[0:1, :] * scale_shift / count

    def masks(c):
        per_point = count_row[0:1, span(c)]
        return [None] + [jnp.where(per_point > k, 1.0, 0.0) for k in range(1, KMAX)]

    def turn_chunk(c):
        part = span(c)
        for copy in dir_copies(c):
            copy.wait()
        own_copy(c).wait()
        speed = (trig[0] * turn_row[2:3, part] - trig[1] * turn_row[1:2, part]) * turn_row[0:1, part]
        face = 0.5 * (speed + pltpu.roll(speed, rows - 1, 0))
        down = jnp.maximum(face, 0.0)
        up = jnp.minimum(face, 0.0)
        active = masks(c)

        def one(f):
            pieces = [own[f, :, part], upper[f, :, part]]
            spare = rows - dir_local - 2 * HALO
            if spare:
                pieces.append(jnp.zeros((spare, CHUNK), jnp.float32))
            pieces.append(lower[f, :, part])
            cells = jnp.concatenate(pieces, axis=0)
            rate = refraction_ref[pl.ds(f, 1), part]
            for k in range(KMAX):
                flux = down * cells + up * pltpu.roll(cells, rows - 1, 0)
                step = rate if k == 0 else rate * active[k]
                cells = cells - step * (flux - pltpu.roll(flux, 1, 0))
            ext[HALO + f, :, part] = cells[:dir_local]

        for f in range(HALO):
            one(f)
            one(freq_local - HALO + f)

        @pl.loop(HALO, freq_local - HALO, step=2)
        def _(f):
            one(f)
            one(f + 1)

        start_pair(freq_copies(c))

    def shift_chunk(c):
        part = span(c)
        wait_pair(freq_copies(c))
        speed = (
            trig[1, :dir_local] * shift_row[2:3, part] + trig[0, :dir_local] * shift_row[1:2, part]
        ) * shift_row[3:4, part]
        high = jnp.maximum(speed, 0.0)
        low = jnp.minimum(speed, 0.0)
        active = masks(c)
        wet_part = shift_row[0:1, part]
        for k in range(KMAX):
            high_k = high if k == 0 else high * active[k]
            low_k = low if k == 0 else low * active[k]

            def flux_at(j, here, there):
                return face_shift[pl.ds(j, 1), part] * (high_k * here + low_k * there)

            here = ext[k + 1, :, part]
            flux = flux_at(k, ext[k, :, part], here)

            def step(j, carry):
                here, flux = carry
                there = ext[j + 1, :, part]
                beyond = flux_at(j, here, there)
                cells = here - (beyond - flux)
                if k == KMAX - 1:
                    out_ref[j - HALO, :, part] = cells * wet_part
                else:
                    ext[j, :, part] = cells
                return there, beyond

            lax.fori_loop(k + 1, freq_local + 2 * HALO - 1 - k, step, (here, flux), unroll=2)

    turn_chunk(0)

    @pl.loop(1, chunks)
    def _(c):
        turn_chunk(c)
        shift_chunk(c - 1)

    shift_chunk(chunks - 1)


def local(mesh, action, bathymetry, refraction, shifting, heading, slope_angle, wet_mask, substeps):
    freq_local, dir_local, points = action.shape
    n_pts, n_dir, n_freq = mesh.shape["pts"], mesh.shape["dir"], mesh.shape["freq"]
    chunks = points // CHUNK
    rows = -(-(dir_local + 2 * HALO) // SUB) * SUB
    group = n_pts * n_freq
    vmem = pl.BlockSpec(memory_space=pltpu.VMEM)
    dma = pltpu.SemaphoreType.DMA
    return pl.pallas_call(
        functools.partial(kernel, n_pts, n_dir, n_freq),
        out_shape=jax.ShapeDtypeStruct(action.shape, jnp.float32),
        in_specs=[pl.BlockSpec(memory_space=pltpu.HBM)] + [vmem] * 7,
        out_specs=vmem,
        scratch_shapes=[
            pltpu.VMEM((freq_local, dir_local, points), jnp.float32),
            pltpu.VMEM((freq_local, HALO, points), jnp.float32),
            pltpu.VMEM((freq_local, HALO, points), jnp.float32),
            pltpu.VMEM((freq_local + 2 * HALO, dir_local, points), jnp.float32),
            pltpu.VMEM((2, SUB, points), jnp.float32),
            pltpu.VMEM((freq_local + 2 * HALO, points), jnp.float32),
            pltpu.VMEM((SUB, points), jnp.float32),
            pltpu.VMEM((SUB, points), jnp.float32),
            pltpu.VMEM((SUB, points), jnp.float32),
            pltpu.VMEM((2, rows, CHUNK), jnp.float32),
            pltpu.VMEM((2, 1, 128), jnp.float32),
            pltpu.VMEM((group, SUB, 128), jnp.float32),
            dma((chunks,)),
            dma((2, chunks)),
            dma((2, chunks)),
            dma((2, chunks)),
            dma((2, chunks)),
            dma((2,)),
            dma((2,)),
            dma((2,)),
            dma((2,)),
            dma((group,)),
            dma((group,)),
        ],
        compiler_params=pltpu.CompilerParams(
            collective_id=0, has_side_effects=True, vmem_limit_bytes=44 * 1024 * 1024
        ),
    )(
        action,
        bathymetry.reshape(1, points),
        refraction,
        shifting,
        heading.reshape(1, points),
        slope_angle.reshape(1, points),
        wet_mask.reshape(1, points),
        substeps.reshape(1, -1),
    )


def solution(mesh):
    placed = (
        P("freq", "dir", "pts"),
        P("pts"),
        P("freq", "pts"),
        P("freq", "pts"),
        P("pts"),
        P("pts"),
        P("pts"),
        P("pts"),
    )
    return jax.shard_map(
        functools.partial(local, mesh),
        mesh=mesh,
        in_specs=placed,
        out_specs=P("freq", "dir", "pts"),
        check_vma=False,
    )
```

profile of v0, /device:TPU:0, one launch (start us, length us, event | category | flops | bytes accessed | tf_op | source)
XLA Modules:
  0.0 89.2 jit_solution(169305683251071425)
XLA Ops:
  0.0 0.0 copy-start
  0.0 1.0 %copy-done = f32[24,4096]{1,0:T(8,128)S(1)} copy-done((f32[24,4096]{1,0:T(8,128)S(1)}, f32[24,4096]{1,0:T(8,128)}, u32[]{:S(2)}) %copy-start) | copy-done | bytes 393240
  1.0 0.0 copy-start.1
  1.0 1.0 %copy-done.1 = f32[24,4096]{1,0:T(8,128)S(1)} copy-done((f32[24,4096]{1,0:T(8,128)S(1)}, f32[24,4096]{1,0:T(8,128)}, u32[]{:S(2)}) %copy-start.1) | copy-done | bytes 393240
  2.0 0.0 copy-start.2
  2.0 0.7 copy-done.2
  2.7 0.0 copy-start.3
  2.7 0.7 copy-done.3
  3.4 0.0 copy-start.4
  3.4 0.7 copy-done.4
  4.1 0.0 copy-start.5
  4.1 0.7 copy-done.5
  4.9 0.0 copy-start.6
  4.9 0.7 copy-done.6
  5.5 81.0 %shard_map.82 = f32[24,16,4096]{2,1,0:T(8,128)S(1)} custom-call(f32[24,16,4096]{2,1,0:T(8,128)} %action_ref.1, f32[1,4096]{1,0:T(1,128)S(1)} %bitcast.5, f32[24,4096]{1,0:T(8,128)S(1)} %copy-done, f32[24,4096]{1,0:T(8,128)S(1)} %copy-done.1, f32[1,4096]{1,0:T(1,128)S(1)} %bitcast.6, f32[1,4096]{1,0:T(1,128)S(1)} %bitcast.7, s32[1,4096]{1,0:T(1,128)S(1)} %bitcast.8, ...), custom_call_target="tpu_custom_call" | custom-call | tf_op jit(solution)/shard_map/pallas_call | solution.py:388
  86.5 2.7 %copy.10 = f32[24,16,4096]{2,1,0:T(8,128)} copy(f32[24,16,4096]{2,1,0:T(8,128)S(1)} %shard_map.82) | data formatting | bytes 12582912
Async XLA Ops:
  0.0 1.0 %copy-start = (f32[24,4096]{1,0:T(8,128)S(1)}, f32[24,4096]{1,0:T(8,128)}, u32[]{:S(2)}) copy-start(f32[24,4096]{1,0:T(8,128)} %refraction_ref.1) | copy-start | bytes 1179652
  1.0 1.0 %copy-start.1 = (f32[24,4096]{1,0:T(8,128)S(1)}, f32[24,4096]{1,0:T(8,128)}, u32[]{:S(2)}) copy-start(f32[24,4096]{1,0:T(8,128)} %shifting_ref.1) | copy-start | bytes 1179652
  2.0 0.7 copy-start.2
  2.7 0.7 copy-start.3
  3.4 0.7 copy-start.4
  4.1 0.7 copy-start.5
  4.9 0.7 copy-start.6
where the time goes:
time: 89.8 us; the launch traced here: 89.2 us
  Pallas kernels  81 us (90%)
  local copies, waits for them, and re-layouts  8.22 us (9%)
    pallas_call x1, Pallas kernels, local(): pl.pallas_call(functools.partial(kernel, n_pts, n_dir, n_freq), out_shape...  81 us
    unnamed x15, local copies, waits for them, and re-layouts  8.22 us

commit v1 on v0

v1 whole, which is shorter than its diff:
```python
import functools
import math

import jax
import jax.numpy as jnp
from jax import lax
from jax.experimental import pallas as pl
from jax.experimental.pallas import tpu as pltpu
from jax.sharding import PartitionSpec as P

FREQ = 48
DIR = 64
KMAX = 4
BLK = 512
CHUNK = 256
LANES = 128
HALO = KMAX
SUB = 8
PIECES = 4

EPSILON = 1e-06
MESH = pl.DeviceIdType.MESH


def turn_row_of(f, part, own, halo, refraction, face, forward, active, rows, dir_local):
    spare = rows - dir_local - 2 * HALO
    if spare:
        cells = jnp.concatenate(
            [
                own[f, :, part],
                halo[f, :HALO, part],
                jnp.zeros((spare, face.shape[1]), jnp.float32),
                halo[f, HALO:, part],
            ],
            axis=0,
        )
    else:
        cells = jnp.concatenate([own[f, :, part], halo[f, :, part]], axis=0)
    rate = refraction[pl.ds(f, 1), part]
    for k in range(KMAX):
        flux = face * jnp.where(forward, cells, pltpu.roll(cells, rows - 1, 0))
        step = rate if k == 0 else rate * active[k]
        cells = cells - step * (flux - pltpu.roll(flux, 1, 0))
    return cells[:dir_local]


def shift_columns(part, ext, face_at, speed, wet, store, size):
    forward = speed > 0.0
    here, flux, out = [None] * KMAX, [None] * KMAX, [None] * KMAX

    def advance(t, k, there, skip_out=False):
        q = t - 2 * k
        beyond = face_at(k, q) * (speed * jnp.where(forward, here[k], there))
        cells = None if skip_out else here[k] - (beyond - flux[k])
        here[k], flux[k] = there, beyond
        return cells

    def ramp(t):
        before = list(out)
        for k in range(KMAX):
            q = t - 2 * k
            if q < k - 1 or q > size - 2 - k:
                continue
            there = ext[q + 1, :, part] if k == 0 else before[k - 1]
            if q == k - 1:
                here[k] = there
            elif q == k:
                advance(t, k, there, skip_out=True)
            else:
                out[k] = advance(t, k, there)
                if k == KMAX - 1:
                    store(q - HALO, out[k] * wet)

    here[0] = ext[0, :, part]
    first = 3 * (KMAX - 1) + 1
    last = size - 1
    for t in range(first):
        ramp(t)

    def step(t, carry):
        now_here, now_flux, now_out = carry
        here[:], flux[:] = list(now_here), list(now_flux)
        fresh = []
        for k in range(KMAX):
            there = ext[t + 1, :, part] if k == 0 else now_out[k - 1]
            fresh.append(advance(t, k, there))
        store(t - 2 * (KMAX - 1) - HALO, fresh[KMAX - 1] * wet)
        return tuple(here), tuple(flux), tuple(fresh[: KMAX - 1])

    trips = last - first
    unroll = 3 if trips % 3 == 0 else 1
    state = lax.fori_loop(first, last, step, (tuple(here), tuple(flux), tuple(out[: KMAX - 1])), unroll=unroll)
    here[:], flux[:], out[: KMAX - 1] = list(state[0]), list(state[1]), list(state[2])
    for t in range(last, size - KMAX + 2 * (KMAX - 1)):
        ramp(t)


def kernel(
    n_pts,
    n_dir,
    n_freq,
    action_ref,
    depth_hbm,
    refraction_hbm,
    shifting_hbm,
    heading_hbm,
    slope_hbm,
    wet_hbm,
    substeps_hbm,
    out_ref,
    tail_own,
    tail_halo,
    tail_ext,
    tail_refraction,
    tail_face,
    tail_speed,
    tail_steps,
    tail_rows,
    own,
    halo,
    ext,
    shext,
    face_shift,
    depth_ref,
    refraction_ref,
    shifting_ref,
    heading_ref,
    slope_ref,
    wet_ref,
    substeps_ref,
    turn_row,
    shift_row,
    count_row,
    trig,
    depth_in,
    peaks,
    own_sem,
    load_sem,
    edge_send,
    edge_recv,
    dir_send,
    dir_recv,
    freq_send,
    freq_recv,
    sh_send,
    sh_recv,
    depth_send,
    depth_recv,
    peak_send,
    peak_recv,
):
    freq_local, dir_local, points = own.shape
    chunks = points // CHUNK
    piece = points // PIECES
    rows = -(-(dir_local + 2 * HALO) // SUB) * SUB
    pts_at = lax.axis_index("pts")
    dir_at = lax.axis_index("dir")
    freq_at = lax.axis_index("freq")
    dir_up, dir_down = lax.rem(dir_at + 1, n_dir), lax.rem(dir_at + n_dir - 1, n_dir)
    pts_up, pts_down = lax.rem(pts_at + 1, n_pts), lax.rem(pts_at + n_pts - 1, n_pts)
    group = n_pts * n_freq
    member = pts_at * n_freq + freq_at
    has_above = freq_at < n_freq - 1
    has_below = freq_at > 0

    def peer(offset):
        other = lax.rem(member + offset, group)
        return {"pts": other // n_freq, "freq": lax.rem(other, n_freq)}

    barrier = pltpu.get_barrier_semaphore()
    for target in (dir_up, dir_down):
        pl.semaphore_signal(barrier, inc=1, device_id={"dir": target}, device_id_type=MESH)
    for offset in range(1, group):
        pl.semaphore_signal(barrier, inc=1, device_id=peer(offset), device_id_type=MESH)

    loads = [
        pltpu.make_async_copy(source, target, load_sem.at[i])
        for i, (source, target) in enumerate(
            (
                (slope_hbm, slope_ref),
                (heading_hbm, heading_ref),
                (depth_hbm, depth_ref),
                (wet_hbm, wet_ref),
                (refraction_hbm, refraction_ref),
                (shifting_hbm, shifting_ref),
                (substeps_hbm, substeps_ref),
            )
        )
    ]
    for copy in loads:
        copy.start()

    def own_copy(i):
        at = pl.ds(pl.multiple_of(i * piece, piece), piece)
        return pltpu.make_async_copy(action_ref.at[:, :, at], own.at[:, :, at], own_sem.at[i])

    for i in range(PIECES):
        own_copy(i).start()

    if n_freq == 1:
        edges = []
        inner, inner_size = 0, freq_local
    elif n_freq == 2:
        edges = [jnp.where(has_above, freq_local - HALO, 0)]
        inner, inner_size = jnp.where(has_above, 0, HALO), freq_local - HALO
    else:
        edges = [0, freq_local - HALO]
        inner, inner_size = HALO, freq_local - 2 * HALO

    def span(c):
        return pl.ds(pl.multiple_of(c * CHUNK, CHUNK), CHUNK)

    def piece_span(i):
        return pl.ds(pl.multiple_of(i * piece, piece), piece)

    def remote(src, dst, send, recv, where):
        return pltpu.make_async_remote_copy(
            src_ref=src, dst_ref=dst, send_sem=send, recv_sem=recv, device_id=where, device_id_type=MESH
        )

    def depth_copies():
        return (
            remote(
                depth_hbm.at[:, pl.ds(points - LANES, LANES)],
                depth_in.at[0],
                depth_send.at[0],
                depth_recv.at[0],
                {"pts": pts_up},
            ),
            remote(
                depth_hbm.at[:, pl.ds(0, LANES)],
                depth_in.at[1],
                depth_send.at[1],
                depth_recv.at[1],
                {"pts": pts_down},
            ),
        )

    def halo_copies(freqs, at, sends, recvs):
        return (
            remote(
                action_ref.at[freqs, pl.ds(dir_local - HALO, HALO), at],
                halo.at[freqs, pl.ds(HALO, HALO), at],
                sends[0],
                recvs[0],
                {"dir": dir_up},
            ),
            remote(
                action_ref.at[freqs, pl.ds(0, HALO), at],
                halo.at[freqs, pl.ds(0, HALO), at],
                sends[1],
                recvs[1],
                {"dir": dir_down},
            ),
        )

    def edge_copies(e, i):
        return halo_copies(
            pl.ds(edges[e], HALO),
            piece_span(i),
            [edge_send.at[way, e, i] for way in range(2)],
            [edge_recv.at[way, e, i] for way in range(2)],
        )

    def dir_copies(c):
        return halo_copies(
            pl.ds(inner, inner_size),
            span(c),
            [dir_send.at[way, c] for way in range(2)],
            [dir_recv.at[way, c] for way in range(2)],
        )

    above, below = lax.rem(freq_at + 1, n_freq), lax.rem(freq_at + n_freq - 1, n_freq)

    def rise(src, dst, send, recv):
        return remote(src, dst, send, recv, {"freq": above})

    def fall(src, dst, send, recv):
        return remote(src, dst, send, recv, {"freq": below})

    def freq_copies(i):
        at = piece_span(i)
        return (
            rise(
                ext.at[pl.ds(freq_local, HALO), :, at],
                ext.at[pl.ds(0, HALO), :, at],
                freq_send.at[0, i],
                freq_recv.at[0, i],
            ),
            fall(
                ext.at[pl.ds(HALO, HALO), :, at],
                ext.at[pl.ds(freq_local + HALO, HALO), :, at],
                freq_send.at[1, i],
                freq_recv.at[1, i],
            ),
        )

    def sh_copies():
        return (
            rise(
                shifting_hbm.at[pl.ds(freq_local - SUB, SUB)],
                shext.at[0],
                sh_send.at[0],
                sh_recv.at[0],
            ),
            fall(shifting_hbm.at[pl.ds(0, SUB)], shext.at[1], sh_send.at[1], sh_recv.at[1]),
        )

    def start_pair(pair):
        @pl.when(has_above)
        def _():
            pair[0].start()

        @pl.when(has_below)
        def _():
            pair[1].start()

    def wait_pair(pair):
        @pl.when(has_above)
        def _():
            pair[0].wait_send()
            pair[1].wait_recv()

        @pl.when(has_below)
        def _():
            pair[1].wait_send()
            pair[0].wait_recv()

    pl.semaphore_wait(barrier, 2 + group - 1)
    for copy in depth_copies():
        copy.start()
    for i in range(PIECES):
        for e in range(len(edges)):
            for copy in edge_copies(e, i):
                copy.start()

    @pl.loop(0, chunks)
    def _(c):
        for copy in dir_copies(c):
            copy.start()

    if n_freq > 1:
        start_pair(sh_copies())

    row = lax.broadcasted_iota(jnp.int32, (rows, CHUNK), 0)
    offset = jnp.where(row >= rows - HALO, row - rows, row)
    angle = ((dir_at * dir_local + offset).astype(jnp.float32) + 0.5) * (2.0 * math.pi / DIR)
    trig[0] = jnp.sin(angle)
    trig[1] = jnp.cos(angle)
    half = lax.broadcasted_iota(jnp.int32, (DIR // 2, LANES), 0)
    half_angle = (half.astype(jnp.float32) + 0.5) * (2.0 * math.pi / DIR)
    half_sin, half_cos = jnp.sin(half_angle), jnp.cos(half_angle)
    for copy in loads:
        copy.wait()
    wet = wet_ref[...].astype(jnp.float32)
    trig_row = (jnp.sin(slope_ref[...]), jnp.cos(slope_ref[...]), jnp.sin(heading_ref[...]), jnp.cos(heading_ref[...]))
    turn_row[1:2, :] = trig_row[0]
    turn_row[2:3, :] = trig_row[1]
    shift_row[1:2, :] = trig_row[2]
    shift_row[2:3, :] = trig_row[3]

    @pl.when(jnp.logical_not(has_below))
    def _():
        @pl.loop(0, HALO)
        def _(f):
            ext[f] = jnp.zeros((dir_local, points), jnp.float32)

    @pl.when(jnp.logical_not(has_above))
    def _():
        @pl.loop(freq_local + HALO, freq_local + 2 * HALO)
        def _(f):
            ext[f] = jnp.zeros((dir_local, points), jnp.float32)

    for copy in depth_copies():
        copy.wait()
    depth = depth_ref[...]
    lane = lax.broadcasted_iota(jnp.int32, (1, points), 1)
    before = jnp.where(pts_at == 0, depth[:, :1], depth_in[0][:, LANES - 1 :])
    after = jnp.where(pts_at == n_pts - 1, depth[:, points - 1 :], depth_in[1][:, :1])
    left = jnp.where(lane == 0, before, pltpu.roll(depth, 1, 1))
    right = jnp.where(lane == points - 1, after, pltpu.roll(depth, points - 1, 1))
    slope = (right - left) * 0.5 * wet
    turn_row[0:1, :] = slope
    shift_row[0:1, :] = wet

    def peak_step(i, carry):
        turn, shift = carry
        part = pl.ds(pl.multiple_of(i * LANES, LANES), LANES)
        sines = jnp.abs(half_sin * turn_row[2:3, part] - half_cos * turn_row[1:2, part])
        cosines = jnp.abs(half_cos * shift_row[2:3, part] + half_sin * shift_row[1:2, part])
        turn_peak = jnp.max(sines, axis=0, keepdims=True) * jnp.abs(turn_row[0:1, part])
        shift_peak = jnp.max(cosines, axis=0, keepdims=True) * shift_row[0:1, part]
        turn = jnp.maximum(turn, jnp.abs(refraction_ref[:, part]) * turn_peak)
        shift = jnp.maximum(shift, jnp.abs(shifting_ref[:, part]) * shift_peak)
        return turn, shift

    zero = jnp.zeros((freq_local, LANES), jnp.float32)
    turn, shift = lax.fori_loop(0, points // LANES, peak_step, (zero, zero))
    turn = jnp.max(jnp.max(turn, axis=0, keepdims=True), axis=1, keepdims=True)
    shift = jnp.max(jnp.max(shift, axis=0, keepdims=True), axis=1, keepdims=True)
    tile = lax.broadcasted_iota(jnp.int32, (SUB, LANES), 0)
    peaks[member] = jnp.where(tile < SUB // 2, turn, shift)

    def peak_copy(offset):
        return remote(
            peaks.at[member], peaks.at[member], peak_send.at[offset], peak_recv.at[offset], peer(offset)
        )

    def peak_arrival(offset):
        source = lax.rem(member + group - offset, group)
        return remote(
            peaks.at[source], peaks.at[source], peak_send.at[offset], peak_recv.at[offset], peer(offset)
        )

    for offset in range(1, group):
        peak_copy(offset).start()

    for block in range(points // BLK):
        part = pl.ds(block * BLK, BLK)
        count_row[0:1, part] = jnp.broadcast_to(
            substeps_ref[0:1, block : block + 1].astype(jnp.float32), (1, BLK)
        )
    count = count_row[0:1, :]
    for k in range(1, KMAX):
        count_row[k : k + 1, :] = jnp.where(count > k, 1.0, 0.0)

    if n_freq > 1:
        wait_pair(sh_copies())
    face_rows = freq_local + 2 * HALO
    first = freq_at * freq_local - HALO

    @pl.loop(0, points // CHUNK)
    def _(c):
        part = span(c)
        window = jnp.concatenate(
            [shext[0, :, part][SUB - HALO :], shifting_ref[:, part], shext[1, :, part][:HALO]], axis=0
        )
        following = jnp.concatenate([window[1:], window[:1]], axis=0)
        mark = first + lax.broadcasted_iota(jnp.int32, (face_rows, CHUNK), 0)
        valid = (mark >= 0) & (mark + 1 <= FREQ - 1)
        face = jnp.where(valid, 0.5 * (window + following), 0.0)
        face_shift[:face_rows, :, part] = face[:, None, :]
        for k in range(1, KMAX):
            face_shift[k * face_rows : (k + 1) * face_rows, :, part] = (face * count_row[k : k + 1, part])[:, None, :]

    for offset in range(1, group):
        peak_copy(offset).wait_send()
        peak_arrival(offset).wait_recv()
    top = jnp.max(peaks[...], axis=0)
    scale_turn = 0.5 / (top[0:1, 0:1] + EPSILON)
    scale_shift = 0.5 / (top[SUB // 2 : SUB // 2 + 1, 0:1] + EPSILON)
    turn_row[0:1, :] = turn_row[0:1, :] * scale_turn / count
    shift_row[3:4, :] = shift_row[0:1, :] * scale_shift / count

    def active_of(part):
        return [None] + [count_row[k : k + 1, part] for k in range(1, KMAX)]

    def turn_face(part):
        speed = (trig[0] * turn_row[2:3, part] - trig[1] * turn_row[1:2, part]) * turn_row[0:1, part]
        return 0.5 * (speed + pltpu.roll(speed, rows - 1, 0))

    def shift_speed(part):
        width = part.size
        return (
            trig[1, :dir_local, :width] * shift_row[2:3, part] + trig[0, :dir_local, :width] * shift_row[1:2, part]
        ) * shift_row[3:4, part]

    def turn_some(c, start, size):
        part = span(c)
        face = turn_face(part)
        forward = face > 0.0
        active = active_of(part)

        def one(f):
            ext[HALO + f, :, part] = turn_row_of(
                f, part, own, halo, refraction_ref, face, forward, active, rows, dir_local
            )

        @pl.loop(0, size // 2)
        def _(i):
            one(start + 2 * i)
            one(start + 2 * i + 1)

    def shift_chunk(c):
        @pl.loop(0, CHUNK // LANES)
        def _(h):
            part = pl.ds(pl.multiple_of(c * CHUNK + h * LANES, LANES), LANES)

            def store(f, value):
                out_ref[f, :, part] = value

            shift_columns(
                part,
                ext,
                lambda k, q: face_shift[k * face_rows + q, :, part],
                shift_speed(part),
                shift_row[0:1, part],
                store,
                face_rows,
            )

    per_piece = chunks // PIECES

    @pl.loop(0, PIECES)
    def _(i):
        own_copy(i).wait()
        for e in range(len(edges)):
            for copy in edge_copies(e, i):
                copy.wait()

        @pl.loop(0, per_piece)
        def _(c):
            for start in edges:
                turn_some(i * per_piece + c, start, HALO)

        if n_freq > 1:
            start_pair(freq_copies(i))

    @pl.loop(0, PIECES)
    def _(i):
        if n_freq > 1:
            wait_pair(freq_copies(i))

        @pl.loop(0, jnp.where(i == PIECES - 1, per_piece - 1, per_piece))
        def _(j):
            c = i * per_piece + j
            for copy in dir_copies(c):
                copy.wait()
            turn_some(c, inner, inner_size)
            shift_chunk(c)

    end = span(chunks - 1)
    tail_own[...] = own[:, :, end]
    tail_ext[...] = ext[:, :, end]
    tail_refraction[...] = refraction_ref[:, end]
    tail_face[...] = turn_face(end)
    tail_speed[...] = shift_speed(end)
    tail_steps[...] = face_shift[:, :, end]
    for k in range(1, KMAX):
        tail_rows[k : k + 1, :] = count_row[k : k + 1, end]
    tail_rows[0:1, :] = shift_row[0:1, end]
    for copy in dir_copies(chunks - 1):
        copy.wait()
    tail_halo[...] = halo[:, :, end]


def finish(
    n_freq,
    done,
    tail_own,
    tail_halo,
    tail_ext,
    tail_refraction,
    tail_face,
    tail_speed,
    tail_steps,
    tail_rows,
    out_hbm,
    ext,
    last,
    main_sem,
    last_sem,
):
    freq_local, dir_local, points = done.shape
    width = tail_own.shape[2]
    rows = tail_face.shape[0]
    pieces = main_sem.shape[0]
    each = freq_local // pieces
    head = points - width

    def main_copy(i):
        freqs = pl.ds(i * each, each)
        at = pl.ds(0, head)
        return pltpu.make_async_copy(done.at[freqs, :, at], out_hbm.at[freqs, :, at], main_sem.at[i])

    for i in range(pieces):
        main_copy(i).start()

    freq_at = lax.axis_index("freq")
    if n_freq == 1:
        inner, inner_size = 0, freq_local
    elif n_freq == 2:
        inner, inner_size = jnp.where(freq_at < n_freq - 1, 0, HALO), freq_local - HALO
    else:
        inner, inner_size = HALO, freq_local - 2 * HALO

    ext[...] = tail_ext[...]
    everything = pl.ds(0, width)
    face = tail_face[...]
    forward = face > 0.0
    active = [None] + [tail_rows[k : k + 1, :] for k in range(1, KMAX)]

    def one(f):
        ext[HALO + f] = turn_row_of(
            f, everything, tail_own, tail_halo, tail_refraction, face, forward, active, rows, dir_local
        )

    @pl.loop(0, inner_size // 2)
    def _(i):
        one(inner + 2 * i)
        one(inner + 2 * i + 1)

    @pl.loop(0, width // LANES)
    def _(h):
        part = pl.ds(pl.multiple_of(h * LANES, LANES), LANES)

        def store(f, value):
            last[f, :, part] = value

        shift_columns(
            part,
            ext,
            lambda k, q: tail_steps[k * (freq_local + 2 * HALO) + q, :, part],
            tail_speed[:, part],
            tail_rows[0:1, part],
            store,
            freq_local + 2 * HALO,
        )

    final = pltpu.make_async_copy(last, out_hbm.at[:, :, pl.ds(head, width)], last_sem)
    final.start()
    for i in range(pieces):
        main_copy(i).wait()
    final.wait()


def local(mesh, action, bathymetry, refraction, shifting, heading, slope_angle, wet_mask, substeps):
    freq_local, dir_local, points = action.shape
    n_pts, n_dir, n_freq = mesh.shape["pts"], mesh.shape["dir"], mesh.shape["freq"]
    chunks = points // CHUNK
    rows = -(-(dir_local + 2 * HALO) // SUB) * SUB
    face_rows = freq_local + 2 * HALO
    group = n_pts * n_freq
    vmem = pl.BlockSpec(memory_space=pltpu.VMEM)
    hbm = pl.BlockSpec(memory_space=pltpu.HBM)
    dma = pltpu.SemaphoreType.DMA
    f32 = jnp.float32
    n_edges = max(1, min(2, n_freq - 1))
    shapes = [
        (freq_local, dir_local, points),
        (freq_local, dir_local, CHUNK),
        (freq_local, 2 * HALO, CHUNK),
        (face_rows, dir_local, CHUNK),
        (freq_local, CHUNK),
        (rows, CHUNK),
        (dir_local, CHUNK),
        (KMAX * face_rows, 1, CHUNK),
        (SUB, CHUNK),
    ]
    parts = pl.pallas_call(
        functools.partial(kernel, n_pts, n_dir, n_freq),
        out_shape=[jax.ShapeDtypeStruct(shape, f32) for shape in shapes],
        in_specs=[hbm] * 8,
        out_specs=[vmem] * len(shapes),
        scratch_shapes=[
            pltpu.VMEM((freq_local, dir_local, points), f32),
            pltpu.VMEM((freq_local, 2 * HALO, points), f32),
            pltpu.VMEM((face_rows, dir_local, points), f32),
            pltpu.VMEM((2, SUB, points), f32),
            pltpu.VMEM((KMAX * face_rows, 1, points), f32),
            pltpu.VMEM((1, points), f32),
            pltpu.VMEM((freq_local, points), f32),
            pltpu.VMEM((freq_local, points), f32),
            pltpu.VMEM((1, points), f32),
            pltpu.VMEM((1, points), f32),
            pltpu.VMEM((1, points), jnp.int32),
            pltpu.VMEM((1, points // BLK), jnp.int32),
            pltpu.VMEM((SUB, points), f32),
            pltpu.VMEM((SUB, points), f32),
            pltpu.VMEM((SUB, points), f32),
            pltpu.VMEM((2, rows, CHUNK), f32),
            pltpu.VMEM((2, 1, LANES), f32),
            pltpu.VMEM((group, SUB, LANES), f32),
            dma((PIECES,)),
            dma((7,)),
            dma((2, n_edges, PIECES)),
            dma((2, n_edges, PIECES)),
            dma((2, chunks)),
            dma((2, chunks)),
            dma((2, PIECES)),
            dma((2, PIECES)),
            dma((2,)),
            dma((2,)),
            dma((2,)),
            dma((2,)),
            dma((group,)),
            dma((group,)),
        ],
        compiler_params=pltpu.CompilerParams(
            collective_id=0, has_side_effects=True, vmem_limit_bytes=44 * 1024 * 1024
        ),
    )(
        action,
        bathymetry.reshape(1, points),
        refraction,
        shifting,
        heading.reshape(1, points),
        slope_angle.reshape(1, points),
        wet_mask.reshape(1, points),
        substeps.reshape(1, -1),
    )
    return pl.pallas_call(
        functools.partial(finish, n_freq),
        out_shape=jax.ShapeDtypeStruct(action.shape, f32),
        in_specs=[vmem] * len(shapes),
        out_specs=hbm,
        scratch_shapes=[
            pltpu.VMEM((face_rows, dir_local, CHUNK), f32),
            pltpu.VMEM((freq_local, dir_local, CHUNK), f32),
            dma((6,)),
            dma(()),
        ],
        compiler_params=pltpu.CompilerParams(vmem_limit_bytes=8 * 1024 * 1024),
    )(*parts)


def solution(mesh):
    placed = (
        P("freq", "dir", "pts"),
        P("pts"),
        P("freq", "pts"),
        P("freq", "pts"),
        P("pts"),
        P("pts"),
        P("pts"),
        P("pts"),
    )
    return jax.shard_map(
        functools.partial(local, mesh),
        mesh=mesh,
        in_specs=placed,
        out_specs=P("freq", "dir", "pts"),
        check_vma=False,
    )
```

time: 89.8 us -> 84.9 us (0.945)
  local copies, waits for them, and re-layouts: 8.22 us -> 5.51 us
  Pallas kernels: 81 us -> 78.8 us
    pallas_call x1, Pallas kernels: 81 us -> 76.1 us  [local(): pl.pallas_call(functools.partial(kernel, n_pts, n_dir, n_freq), out_shape...]
    pallas_call x0 -> x1, Pallas kernels: none -> 2.72 us  [local(): pl.pallas_call(functools.partial(finish, n_freq), out_shape=jax.ShapeDtyp...]
    unnamed x15 -> x14, local copies, waits for them, and re-layouts: 8.22 us -> 5.51 us
where the time goes in v1:
time: 84.9 us; the launch traced here: 84.4 us
  Pallas kernels  78.8 us (93%)
  local copies, waits for them, and re-layouts  5.51 us (6%)
    pallas_call x1, Pallas kernels, local(): pl.pallas_call(functools.partial(kernel, n_pts, n_dir, n_freq), out_shape...  76.1 us
    unnamed x14, local copies, waits for them, and re-layouts  5.51 us
    pallas_call x1, Pallas kernels, local(): pl.pallas_call(functools.partial(finish, n_freq), out_shape=jax.ShapeDtyp...  2.72 us

profile of v1, /device:TPU:0, one launch (start us, length us, event | category | flops | bytes accessed | tf_op | source)
XLA Modules:
  0.0 84.4 jit_solution(16560100899250427568)
XLA Ops:
  0.0 0.0 copy-start
  0.0 1.0 %copy-done = f32[24,4096]{1,0:T(8,128)S(1)} copy-done((f32[24,4096]{1,0:T(8,128)S(1)}, f32[24,4096]{1,0:T(8,128)}, u32[]{:S(2)}) %copy-start) | copy-done | bytes 393240
  1.0 0.0 copy-start.1
  1.0 1.0 %copy-done.1 = f32[24,4096]{1,0:T(8,128)S(1)} copy-done((f32[24,4096]{1,0:T(8,128)S(1)}, f32[24,4096]{1,0:T(8,128)}, u32[]{:S(2)}) %copy-start.1) | copy-done | bytes 393240
  2.0 0.0 copy-start.2
  2.0 0.7 copy-done.2
  2.7 0.0 copy-start.3
  2.7 0.7 copy-done.3
  3.4 0.0 copy-start.4
  3.4 0.7 copy-done.4
  4.1 0.0 copy-start.5
  4.1 0.7 copy-done.5
  4.9 0.0 copy-start.6
  4.9 0.7 copy-done.6
  5.5 76.1 %shard_map.82 = (f32[24,16,4096]{2,1,0:T(8,128)S(1)}, f32[24,16,256]{2,1,0:T(8,128)S(1)}, f32[24,8,256]{2,1,0:T(8,128)S(1)}, f32[32,16,256]{2,1,0:T(8,128)S(1)},...) custom-call(f32[24,16,4096]{2,1,0:T(8,128)} %action_ref.1, ...), custom_call_target="tpu_custom_call" | custom-call | tf_op jit(solution)/shard_map/pallas_call | solution.py:650
  81.6 2.7 %shard_map.83 = f32[24,16,4096]{2,1,0:T(8,128)} custom-call(f32[24,16,4096]{2,1,0:T(8,128)S(1)} %get-tuple-element.14.done, f32[24,16,256]{2,1,0:T(8,128)S(1)} %get-tuple-element.15.tail_own, f32[24,8,256]{2,1,0:T(8,128)S(1)} %get-tuple-element.16.tail_halo, f32[32,16,256]{2,1,0:T(8,128)S(1)} %get-tuple-element.17.tail_ext, ...), custom_call_target="tpu_custom_call" | custom-call | tf_op jit(solution)/shard_map/pallas_call | solution.py:702
Async XLA Ops:
  0.0 1.0 %copy-start = (f32[24,4096]{1,0:T(8,128)S(1)}, f32[24,4096]{1,0:T(8,128)}, u32[]{:S(2)}) copy-start(f32[24,4096]{1,0:T(8,128)} %refraction_hbm.1) | copy-start | bytes 1179652
  1.0 1.0 %copy-start.1 = (f32[24,4096]{1,0:T(8,128)S(1)}, f32[24,4096]{1,0:T(8,128)}, u32[]{:S(2)}) copy-start(f32[24,4096]{1,0:T(8,128)} %shifting_hbm.1) | copy-start | bytes 1179652
  2.0 0.7 copy-start.2
  2.7 0.7 copy-start.3
  3.4 0.7 copy-start.4
  4.1 0.7 copy-start.5
  4.9 0.7 copy-start.6

commit v2 on v1

--- a/solution.py
+++ b/solution.py
@@ -690,14 +690,19 @@
             collective_id=0, has_side_effects=True, vmem_limit_bytes=44 * 1024 * 1024
         ),
     )(
-        action,
-        bathymetry.reshape(1, points),
-        refraction,
-        shifting,
-        heading.reshape(1, points),
-        slope_angle.reshape(1, points),
-        wet_mask.reshape(1, points),
-        substeps.reshape(1, -1),
+        *[
+            pltpu.with_memory_space_constraint(array, pltpu.HBM)
+            for array in (
+                action,
+                bathymetry.reshape(1, points),
+                refraction,
+                shifting,
+                heading.reshape(1, points),
+                slope_angle.reshape(1, points),
+                wet_mask.reshape(1, points),
+                substeps.reshape(1, -1),
+            )
+        ]
     )
     return pl.pallas_call(
         functools.partial(finish, n_freq),

time: 84.9 us -> 79 us (0.931)
  local copies, waits for them, and re-layouts: 5.51 us -> 0 us
    unnamed x14 -> x0, local copies, waits for them, and re-layouts: 5.51 us -> none
where the time goes in v2:
time: 79 us; the launch traced here: 78.9 us
  Pallas kernels  78.8 us (100%)
    pallas_call x1, Pallas kernels, local(): pl.pallas_call(functools.partial(kernel, n_pts, n_dir, n_freq), out_shape...  76.1 us
    pallas_call x1, Pallas kernels, local(): pl.pallas_call(functools.partial(finish, n_freq), out_shape=jax.ShapeDtyp...  2.72 us

profile of v2, /device:TPU:0, one launch (start us, length us, event | category | flops | bytes accessed | tf_op | source)
XLA Modules:
  0.0 78.9 jit_solution(16182175361205323080)
XLA Ops:
  0.0 76.1 %shard_map.82 = (f32[24,16,4096]{2,1,0:T(8,128)S(1)}, f32[24,16,256]{2,1,0:T(8,128)S(1)}, f32[24,8,256]{2,1,0:T(8,128)S(1)}, f32[32,16,256]{2,1,0:T(8,128)S(1)},...) custom-call(f32[24,16,4096]{2,1,0:T(8,128)} %action_ref.1, ...), custom_call_target="tpu_custom_call" | custom-call | tf_op jit(solution)/shard_map/pallas_call | solution.py:650
  76.1 2.7 %shard_map.83 = f32[24,16,4096]{2,1,0:T(8,128)} custom-call(f32[24,16,4096]{2,1,0:T(8,128)S(1)} %get-tuple-element.14.done, f32[24,16,256]{2,1,0:T(8,128)S(1)} %get-tuple-element.15.tail_own, f32[24,8,256]{2,1,0:T(8,128)S(1)} %get-tuple-element.16.tail_halo, f32[32,16,256]{2,1,0:T(8,128)S(1)} %get-tuple-element.17.tail_ext, ...), custom_call_target="tpu_custom_call" | custom-call | tf_op jit(solution)/shard_map/pallas_call | solution.py:707

commit v3 on v2

--- a/solution.py
+++ b/solution.py
@@ -17,6 +17,7 @@
 HALO = KMAX
 SUB = 8
 PIECES = 4
+LEAD = 1
 
 EPSILON = 1e-06
 MESH = pl.DeviceIdType.MESH
@@ -93,6 +94,19 @@
     here[:], flux[:], out[: KMAX - 1] = list(state[0]), list(state[1]), list(state[2])
     for t in range(last, size - KMAX + 2 * (KMAX - 1)):
         ramp(t)
+
+
+def peak_stages(n_pts, n_freq):
+    stages = []
+    for axis, count in (("pts", n_pts), ("freq", n_freq)):
+        if count & (count - 1) == 0:
+            amount = 1
+            while amount < count:
+                stages.append([(axis, "swap", amount)])
+                amount *= 2
+        else:
+            stages.append([(axis, "turn", amount) for amount in range(1, count)])
+    return stages
 
 
 def kernel(
@@ -157,21 +171,41 @@
     dir_at = lax.axis_index("dir")
     freq_at = lax.axis_index("freq")
     dir_up, dir_down = lax.rem(dir_at + 1, n_dir), lax.rem(dir_at + n_dir - 1, n_dir)
-    pts_up, pts_down = lax.rem(pts_at + 1, n_pts), lax.rem(pts_at + n_pts - 1, n_pts)
-    group = n_pts * n_freq
-    member = pts_at * n_freq + freq_at
     has_above = freq_at < n_freq - 1
     has_below = freq_at > 0
-
-    def peer(offset):
-        other = lax.rem(member + offset, group)
-        return {"pts": other // n_freq, "freq": lax.rem(other, n_freq)}
+    has_next = pts_at < n_pts - 1
+    has_last = pts_at > 0
+    stages = peak_stages(n_pts, n_freq)
+    places = {"pts": (pts_at, n_pts), "freq": (freq_at, n_freq)}
+
+    def partner(axis, kind, amount):
+        at, count = places[axis]
+        if kind == "swap":
+            return {axis: at + amount * (1 - 2 * lax.rem(lax.div(at, amount), 2))}
+        return {axis: lax.rem(at + amount, count)}
 
     barrier = pltpu.get_barrier_semaphore()
-    for target in (dir_up, dir_down):
-        pl.semaphore_signal(barrier, inc=1, device_id={"dir": target}, device_id_type=MESH)
-    for offset in range(1, group):
-        pl.semaphore_signal(barrier, inc=1, device_id=peer(offset), device_id_type=MESH)
+
+    def greet(where):
+        pl.semaphore_signal(barrier, inc=1, device_id=where, device_id_type=MESH)
+
+    neighbours = [(has_next, {"pts": pts_at + 1}), (has_last, {"pts": pts_at - 1})]
+    if n_freq > 2:
+        neighbours += [(has_above, {"freq": freq_at + 1}), (has_below, {"freq": freq_at - 1})]
+    greet({"dir": dir_up})
+    greet({"dir": dir_down})
+    for stage in stages:
+        for move in stage:
+            greet(partner(*move))
+    for there, where in neighbours:
+        pl.when(there)(functools.partial(greet, where))
+
+    def own_copy(i):
+        at = pl.ds(pl.multiple_of(i * piece, piece), piece)
+        return pltpu.make_async_copy(action_ref.at[:, :, at], own.at[:, :, at], own_sem.at[i])
+
+    for i in range(PIECES):
+        own_copy(i).start()
 
     loads = [
         pltpu.make_async_copy(source, target, load_sem.at[i])
@@ -190,13 +224,6 @@
     for copy in loads:
         copy.start()
 
-    def own_copy(i):
-        at = pl.ds(pl.multiple_of(i * piece, piece), piece)
-        return pltpu.make_async_copy(action_ref.at[:, :, at], own.at[:, :, at], own_sem.at[i])
-
-    for i in range(PIECES):
-        own_copy(i).start()
-
     if n_freq == 1:
         edges = []
         inner, inner_size = 0, freq_local
@@ -218,57 +245,40 @@
             src_ref=src, dst_ref=dst, send_sem=send, recv_sem=recv, device_id=where, device_id_type=MESH
         )
 
-    def depth_copies():
-        return (
-            remote(
-                depth_hbm.at[:, pl.ds(points - LANES, LANES)],
-                depth_in.at[0],
-                depth_send.at[0],
-                depth_recv.at[0],
-                {"pts": pts_up},
-            ),
-            remote(
-                depth_hbm.at[:, pl.ds(0, LANES)],
-                depth_in.at[1],
-                depth_send.at[1],
-                depth_recv.at[1],
-                {"pts": pts_down},
-            ),
-        )
-
-    def halo_copies(freqs, at, sends, recvs):
-        return (
-            remote(
-                action_ref.at[freqs, pl.ds(dir_local - HALO, HALO), at],
-                halo.at[freqs, pl.ds(HALO, HALO), at],
-                sends[0],
-                recvs[0],
-                {"dir": dir_up},
-            ),
-            remote(
-                action_ref.at[freqs, pl.ds(0, HALO), at],
-                halo.at[freqs, pl.ds(0, HALO), at],
-                sends[1],
-                recvs[1],
-                {"dir": dir_down},
-            ),
-        )
-
-    def edge_copies(e, i):
-        return halo_copies(
-            pl.ds(edges[e], HALO),
-            piece_span(i),
-            [edge_send.at[way, e, i] for way in range(2)],
-            [edge_recv.at[way, e, i] for way in range(2)],
-        )
-
-    def dir_copies(c):
-        return halo_copies(
-            pl.ds(inner, inner_size),
-            span(c),
-            [dir_send.at[way, c] for way in range(2)],
-            [dir_recv.at[way, c] for way in range(2)],
-        )
+    def depth_up():
+        return remote(
+            depth_hbm.at[:, pl.ds(points - LANES, LANES)],
+            depth_in.at[0],
+            depth_send.at[0],
+            depth_recv.at[0],
+            {"pts": pts_at + 1},
+        )
+
+    def depth_down():
+        return remote(
+            depth_hbm.at[:, pl.ds(0, LANES)],
+            depth_in.at[1],
+            depth_send.at[1],
+            depth_recv.at[1],
+            {"pts": pts_at - 1},
+        )
+
+    def halo_copy(way, freqs, at, send, recv):
+        top = pl.ds(dir_local - HALO, HALO)
+        source, target, where = (top, pl.ds(HALO, HALO), dir_up) if way == 0 else (
+            pl.ds(0, HALO),
+            pl.ds(0, HALO),
+            dir_down,
+        )
+        return remote(own.at[freqs, source, at], halo.at[freqs, target, at], send, recv, {"dir": where})
+
+    def edge_copy(way, e, i):
+        return halo_copy(
+            way, pl.ds(edges[e], HALO), piece_span(i), edge_send.at[way, e, i], edge_recv.at[way, e, i]
+        )
+
+    def dir_copy(way, c):
+        return halo_copy(way, pl.ds(inner, inner_size), span(c), dir_send.at[way, c], dir_recv.at[way, c])
 
     above, below = lax.rem(freq_at + 1, n_freq), lax.rem(freq_at + n_freq - 1, n_freq)
 
@@ -326,18 +336,49 @@
             pair[1].wait_send()
             pair[0].wait_recv()
 
-    pl.semaphore_wait(barrier, 2 + group - 1)
-    for copy in depth_copies():
-        copy.start()
-    for i in range(PIECES):
-        for e in range(len(edges)):
-            for copy in edge_copies(e, i):
-                copy.start()
-
-    @pl.loop(0, chunks)
-    def _(c):
-        for copy in dir_copies(c):
-            copy.start()
+    beside = jnp.minimum(pts_at, 1) + jnp.minimum(n_pts - 1 - pts_at, 1)
+    if n_freq > 2:
+        beside += jnp.minimum(freq_at, 1) + jnp.minimum(n_freq - 1 - freq_at, 1)
+    pl.semaphore_wait(barrier, 2 + sum(len(stage) for stage in stages) + beside)
+
+    @pl.when(has_next)
+    def _():
+        depth_up().start()
+
+    @pl.when(has_last)
+    def _():
+        depth_down().start()
+
+    def start_halos(far):
+        ways = (0, 1) if far is None else (far, 1 - far)
+        ahead = 0 if far is None else LEAD
+        for i in range(PIECES):
+            own_copy(i).wait()
+            for e in range(len(edges)):
+                for way in ways:
+                    edge_copy(way, e, i).start()
+        for c in range(ahead):
+            dir_copy(ways[0], c).start()
+
+        @pl.loop(0, chunks - ahead)
+        def _(c):
+            dir_copy(ways[0], c + ahead).start()
+            dir_copy(ways[1], c).start()
+
+        for c in range(chunks - ahead, chunks):
+            dir_copy(ways[1], c).start()
+
+    @pl.when(dir_at == 0)
+    def _():
+        start_halos(1)
+
+    @pl.when(dir_at == n_dir - 1)
+    def _():
+        start_halos(0)
+
+    @pl.when((dir_at > 0) & (dir_at < n_dir - 1))
+    def _():
+        start_halos(None)
 
     if n_freq > 1:
         start_pair(sh_copies())
@@ -371,8 +412,16 @@
         def _(f):
             ext[f] = jnp.zeros((dir_local, points), jnp.float32)
 
-    for copy in depth_copies():
-        copy.wait()
+    @pl.when(has_next)
+    def _():
+        depth_up().wait_send()
+        depth_down().wait_recv()
+
+    @pl.when(has_last)
+    def _():
+        depth_down().wait_send()
+        depth_up().wait_recv()
+
     depth = depth_ref[...]
     lane = lax.broadcasted_iota(jnp.int32, (1, points), 1)
     before = jnp.where(pts_at == 0, depth[:, :1], depth_in[0][:, LANES - 1 :])
@@ -399,21 +448,19 @@
     turn = jnp.max(jnp.max(turn, axis=0, keepdims=True), axis=1, keepdims=True)
     shift = jnp.max(jnp.max(shift, axis=0, keepdims=True), axis=1, keepdims=True)
     tile = lax.broadcasted_iota(jnp.int32, (SUB, LANES), 0)
-    peaks[member] = jnp.where(tile < SUB // 2, turn, shift)
-
-    def peak_copy(offset):
+    peaks[0] = jnp.where(tile < SUB // 2, turn, shift)
+
+    def peak_copy(source, slot, move):
         return remote(
-            peaks.at[member], peaks.at[member], peak_send.at[offset], peak_recv.at[offset], peer(offset)
-        )
-
-    def peak_arrival(offset):
-        source = lax.rem(member + group - offset, group)
-        return remote(
-            peaks.at[source], peaks.at[source], peak_send.at[offset], peak_recv.at[offset], peer(offset)
-        )
-
-    for offset in range(1, group):
-        peak_copy(offset).start()
+            peaks.at[source], peaks.at[slot], peak_send.at[slot], peak_recv.at[slot], partner(*move)
+        )
+
+    slots, taken = [], 1
+    for stage in stages:
+        slots.append((taken - 1, [(taken + i, move) for i, move in enumerate(stage)]))
+        taken += len(stage) + 1
+    for slot, move in slots[0][1] if slots else []:
+        peak_copy(0, slot, move).start()
 
     for block in range(points // BLK):
         part = pl.ds(block * BLK, BLK)
@@ -443,10 +490,16 @@
         for k in range(1, KMAX):
             face_shift[k * face_rows : (k + 1) * face_rows, :, part] = (face * count_row[k : k + 1, part])[:, None, :]
 
-    for offset in range(1, group):
-        peak_copy(offset).wait_send()
-        peak_arrival(offset).wait_recv()
-    top = jnp.max(peaks[...], axis=0)
+    top = peaks[0]
+    for at, (source, moves) in enumerate(slots):
+        for slot, move in moves:
+            if at:
+                peak_copy(source, slot, move).start()
+        for slot, move in moves:
+            peak_copy(source, slot, move).wait()
+            top = jnp.maximum(top, peaks[slot])
+        if at + 1 < len(slots):
+            peaks[slots[at + 1][0]] = top
     scale_turn = 0.5 / (top[0:1, 0:1] + EPSILON)
     scale_shift = 0.5 / (top[SUB // 2 : SUB // 2 + 1, 0:1] + EPSILON)
     turn_row[0:1, :] = turn_row[0:1, :] * scale_turn / count
@@ -503,10 +556,9 @@
 
     @pl.loop(0, PIECES)
     def _(i):
-        own_copy(i).wait()
         for e in range(len(edges)):
-            for copy in edge_copies(e, i):
-                copy.wait()
+            for way in range(2):
+                edge_copy(way, e, i).wait()
 
         @pl.loop(0, per_piece)
         def _(c):
@@ -524,8 +576,8 @@
         @pl.loop(0, jnp.where(i == PIECES - 1, per_piece - 1, per_piece))
         def _(j):
             c = i * per_piece + j
-            for copy in dir_copies(c):
-                copy.wait()
+            for way in range(2):
+                dir_copy(way, c).wait()
             turn_some(c, inner, inner_size)
             shift_chunk(c)
 
@@ -539,8 +591,8 @@
     for k in range(1, KMAX):
         tail_rows[k : k + 1, :] = count_row[k : k + 1, end]
     tail_rows[0:1, :] = shift_row[0:1, end]
-    for copy in dir_copies(chunks - 1):
-        copy.wait()
+    for way in range(2):
+        dir_copy(way, chunks - 1).wait()
     tail_halo[...] = halo[:, :, end]
 
 
@@ -630,7 +682,7 @@
     chunks = points // CHUNK
     rows = -(-(dir_local + 2 * HALO) // SUB) * SUB
     face_rows = freq_local + 2 * HALO
-    group = n_pts * n_freq
+    n_slots = 1 + sum(len(stage) + 1 for stage in peak_stages(n_pts, n_freq))
     vmem = pl.BlockSpec(memory_space=pltpu.VMEM)
     hbm = pl.BlockSpec(memory_space=pltpu.HBM)
     dma = pltpu.SemaphoreType.DMA
@@ -670,7 +722,7 @@
             pltpu.VMEM((SUB, points), f32),
             pltpu.VMEM((2, rows, CHUNK), f32),
             pltpu.VMEM((2, 1, LANES), f32),
-            pltpu.VMEM((group, SUB, LANES), f32),
+            pltpu.VMEM((n_slots, SUB, LANES), f32),
             dma((PIECES,)),
             dma((7,)),
             dma((2, n_edges, PIECES)),
@@ -683,8 +735,8 @@
             dma((2,)),
             dma((2,)),
             dma((2,)),
-            dma((group,)),
-            dma((group,)),
+            dma((n_slots,)),
+            dma((n_slots,)),
         ],
         compiler_params=pltpu.CompilerParams(
             collective_id=0, has_side_effects=True, vmem_limit_bytes=44 * 1024 * 1024

time: 79 us -> 77 us (0.975)
  Pallas kernels: 78.8 us -> 76.9 us
    pallas_call x1, Pallas kernels: 76.1 us -> 74.1 us  [local(): pl.pallas_call(functools.partial(kernel, n_pts, n_dir, n_freq), out_shape...]
where the time goes in v3:
time: 77 us; the launch traced here: 76.9 us
  Pallas kernels  76.9 us (100%)
    pallas_call x1, Pallas kernels, local(): pl.pallas_call(functools.partial(kernel, n_pts, n_dir, n_freq), out_shape...  74.1 us
    pallas_call x1, Pallas kernels, local(): pl.pallas_call(functools.partial(finish, n_freq), out_shape=jax.ShapeDtyp...  2.72 us

profile of v3, /device:TPU:0, one launch (start us, length us, event | category | flops | bytes accessed | tf_op | source)
XLA Modules:
  0.0 76.9 jit_solution(521892735601878852)
XLA Ops:
  0.0 74.1 %shard_map.82 = (f32[24,16,4096]{2,1,0:T(8,128)S(1)}, f32[24,16,256]{2,1,0:T(8,128)S(1)}, f32[24,8,256]{2,1,0:T(8,128)S(1)}, f32[32,16,256]{2,1,0:T(8,128)S(1)},...) custom-call(f32[24,16,4096]{2,1,0:T(8,128)} %action_ref.1, ...), custom_call_target="tpu_custom_call" | custom-call | tf_op jit(solution)/shard_map/pallas_call | solution.py:702
  74.1 2.7 %shard_map.83 = f32[24,16,4096]{2,1,0:T(8,128)} custom-call(f32[24,16,4096]{2,1,0:T(8,128)S(1)} %get-tuple-element.14.done, f32[24,16,256]{2,1,0:T(8,128)S(1)} %get-tuple-element.15.tail_own, f32[24,8,256]{2,1,0:T(8,128)S(1)} %get-tuple-element.16.tail_halo, f32[32,16,256]{2,1,0:T(8,128)S(1)} %get-tuple-element.17.tail_ext, ...), custom_call_target="tpu_custom_call" | custom-call | tf_op jit(solution)/shard_map/pallas_call | solution.py:759

commit v4 on v3

--- a/solution.py
+++ b/solution.py
@@ -149,6 +149,7 @@
     depth_in,
     peaks,
     own_sem,
+    own_edge_sem,
     load_sem,
     edge_send,
     edge_recv,
@@ -162,6 +163,9 @@
     depth_recv,
     peak_send,
     peak_recv,
+    dir_ready,
+    stage_ready,
+    next_ready,
 ):
     freq_local, dir_local, points = own.shape
     chunks = points // CHUNK
@@ -184,28 +188,75 @@
             return {axis: at + amount * (1 - 2 * lax.rem(lax.div(at, amount), 2))}
         return {axis: lax.rem(at + amount, count)}
 
+    def bit(axis, amount):
+        return lax.rem(lax.div(places[axis][0], amount), 2)
+
+    neighbours = [(0, has_next, has_last, "pts")]
+    if n_freq > 2:
+        neighbours.append((1, has_above, has_below, "freq"))
     barrier = pltpu.get_barrier_semaphore()
 
     def greet(where):
         pl.semaphore_signal(barrier, inc=1, device_id=where, device_id_type=MESH)
 
-    neighbours = [(has_next, {"pts": pts_at + 1}), (has_last, {"pts": pts_at - 1})]
-    if n_freq > 2:
-        neighbours += [(has_above, {"freq": freq_at + 1}), (has_below, {"freq": freq_at - 1})]
-    greet({"dir": dir_up})
-    greet({"dir": dir_down})
+    last_dir = n_dir - 1
+
+    @pl.when(dir_at < last_dir)
+    def _():
+        greet({"dir": dir_up})
+
+    @pl.when(dir_at == 1)
+    def _():
+        greet({"dir": dir_down})
+
+    @pl.when(dir_at == 0)
+    def _():
+        greet({"dir": dir_down})
+
+    parents = 1 + lax.div(dir_at, last_dir)
     for stage in stages:
-        for move in stage:
-            greet(partner(*move))
-    for there, where in neighbours:
-        pl.when(there)(functools.partial(greet, where))
-
-    def own_copy(i):
-        at = pl.ds(pl.multiple_of(i * piece, piece), piece)
-        return pltpu.make_async_copy(action_ref.at[:, :, at], own.at[:, :, at], own_sem.at[i])
+        for axis, kind, amount in stage:
+            if kind == "swap":
+                pl.when(bit(axis, amount) == 0)(functools.partial(greet, partner(axis, kind, amount)))
+                parents += bit(axis, amount)
+            else:
+                greet(partner(axis, kind, amount))
+                parents += 1
+    for _, up_there, _, axis in neighbours:
+        pl.when(up_there)(functools.partial(greet, {axis: places[axis][0] + 1}))
+        parents += jnp.minimum(places[axis][0], 1)
+
+    if n_freq == 1:
+        edges = []
+        inner, inner_size = 0, freq_local
+    elif n_freq == 2:
+        edges = [jnp.where(has_above, freq_local - HALO, 0)]
+        inner, inner_size = jnp.where(has_above, 0, HALO), freq_local - HALO
+    else:
+        edges = [0, freq_local - HALO]
+        inner, inner_size = HALO, freq_local - 2 * HALO
+
+    def span(c):
+        return pl.ds(pl.multiple_of(c * CHUNK, CHUNK), CHUNK)
+
+    def piece_span(i):
+        return pl.ds(pl.multiple_of(i * piece, piece), piece)
+
+    def own_part(freqs, i, sem):
+        at = piece_span(i)
+        return pltpu.make_async_copy(action_ref.at[freqs, :, at], own.at[freqs, :, at], sem)
+
+    def own_edge(e, i):
+        return own_part(pl.ds(edges[e], HALO), i, own_edge_sem.at[e, i])
+
+    def own_inner(i):
+        return own_part(pl.ds(inner, inner_size), i, own_sem.at[i])
 
     for i in range(PIECES):
-        own_copy(i).start()
+        for e in range(len(edges)):
+            own_edge(e, i).start()
+    for i in range(PIECES):
+        own_inner(i).start()
 
     loads = [
         pltpu.make_async_copy(source, target, load_sem.at[i])
@@ -223,22 +274,6 @@
     ]
     for copy in loads:
         copy.start()
-
-    if n_freq == 1:
-        edges = []
-        inner, inner_size = 0, freq_local
-    elif n_freq == 2:
-        edges = [jnp.where(has_above, freq_local - HALO, 0)]
-        inner, inner_size = jnp.where(has_above, 0, HALO), freq_local - HALO
-    else:
-        edges = [0, freq_local - HALO]
-        inner, inner_size = HALO, freq_local - 2 * HALO
-
-    def span(c):
-        return pl.ds(pl.multiple_of(c * CHUNK, CHUNK), CHUNK)
-
-    def piece_span(i):
-        return pl.ds(pl.multiple_of(i * piece, piece), piece)
 
     def remote(src, dst, send, recv, where):
         return pltpu.make_async_remote_copy(
@@ -336,49 +371,111 @@
             pair[1].wait_send()
             pair[0].wait_recv()
 
-    beside = jnp.minimum(pts_at, 1) + jnp.minimum(n_pts - 1 - pts_at, 1)
-    if n_freq > 2:
-        beside += jnp.minimum(freq_at, 1) + jnp.minimum(n_freq - 1 - freq_at, 1)
-    pl.semaphore_wait(barrier, 2 + sum(len(stage) for stage in stages) + beside)
-
-    @pl.when(has_next)
-    def _():
-        depth_up().start()
-
-    @pl.when(has_last)
-    def _():
-        depth_down().start()
-
-    def start_halos(far):
-        ways = (0, 1) if far is None else (far, 1 - far)
-        ahead = 0 if far is None else LEAD
-        for i in range(PIECES):
-            own_copy(i).wait()
+    def report(sem, where):
+        pl.semaphore_signal(sem, inc=1, device_id=where, device_id_type=MESH)
+
+    pl.semaphore_wait(barrier, parents)
+
+    @pl.when(dir_at > 1)
+    def _():
+        report(dir_ready, {"dir": dir_down})
+
+    @pl.when(dir_at == last_dir)
+    def _():
+        report(dir_ready, {"dir": dir_up})
+
+    for at, stage in enumerate(stages):
+        for axis, kind, amount in stage:
+            if kind == "swap":
+                below_there = bit(axis, amount) == 1
+                pl.when(below_there)(functools.partial(report, stage_ready.at[at], partner(axis, kind, amount)))
+    for i, up_there, down_there, axis in neighbours:
+        pl.when(down_there)(functools.partial(report, next_ready.at[i], {axis: places[axis][0] - 1}))
+    def start_edges(way, low=0, high=PIECES):
+        for i in range(low, high):
             for e in range(len(edges)):
-                for way in ways:
-                    edge_copy(way, e, i).start()
+                edge_copy(way, e, i).start()
+
+    def start_inner(first, ahead):
         for c in range(ahead):
-            dir_copy(ways[0], c).start()
+            dir_copy(first, c).start()
 
         @pl.loop(0, chunks - ahead)
         def _(c):
-            dir_copy(ways[0], c + ahead).start()
-            dir_copy(ways[1], c).start()
+            dir_copy(first, c + ahead).start()
+            dir_copy(1 - first, c).start()
 
         for c in range(chunks - ahead, chunks):
-            dir_copy(ways[1], c).start()
+            dir_copy(1 - first, c).start()
+
+    for i in range(PIECES):
+        for e in range(len(edges)):
+            own_edge(e, i).wait()
+
+    is_end = (dir_at == 0) | (dir_at == last_dir)
 
     @pl.when(dir_at == 0)
     def _():
-        start_halos(1)
-
-    @pl.when(dir_at == n_dir - 1)
-    def _():
-        start_halos(0)
-
-    @pl.when((dir_at > 0) & (dir_at < n_dir - 1))
-    def _():
-        start_halos(None)
+        start_edges(0, 0, 1)
+
+    @pl.when(dir_at == last_dir)
+    def _():
+        start_edges(0, 0, 1)
+
+    @pl.when(jnp.logical_not(is_end))
+    def _():
+        start_edges(1)
+
+
+    @pl.when(dir_at < last_dir)
+    def _():
+        pl.semaphore_wait(dir_ready, 1)
+
+    for i in range(PIECES):
+        own_inner(i).wait()
+
+    @pl.when(dir_at == 0)
+    def _():
+        for i in range(PIECES):
+            start_edges(1, i, i + 1)
+            if i + 1 < PIECES:
+                start_edges(0, i + 1, i + 2)
+        start_inner(1, LEAD)
+
+    @pl.when(dir_at == last_dir)
+    def _():
+        for i in range(PIECES):
+            start_edges(1, i, i + 1)
+            if i + 1 < PIECES:
+                start_edges(0, i + 1, i + 2)
+        start_inner(0, LEAD)
+
+    @pl.when(jnp.logical_not(is_end))
+    def _():
+        start_edges(0)
+        start_inner(0, 0)
+
+    for at, stage in enumerate(stages):
+        for axis, kind, amount in stage:
+            if kind == "swap":
+
+                @pl.when(bit(axis, amount) == 0)
+                def _():
+                    pl.semaphore_wait(stage_ready.at[at], 1)
+
+    for i, up_there, down_there, axis in neighbours:
+
+        @pl.when(up_there)
+        def _():
+            pl.semaphore_wait(next_ready.at[i], 1)
+
+    @pl.when(has_next)
+    def _():
+        depth_up().start()
+
+    @pl.when(has_last)
+    def _():
+        depth_down().start()
 
     if n_freq > 1:
         start_pair(sh_copies())
@@ -682,7 +779,8 @@
     chunks = points // CHUNK
     rows = -(-(dir_local + 2 * HALO) // SUB) * SUB
     face_rows = freq_local + 2 * HALO
-    n_slots = 1 + sum(len(stage) + 1 for stage in peak_stages(n_pts, n_freq))
+    stages = peak_stages(n_pts, n_freq)
+    n_slots = 1 + sum(len(stage) + 1 for stage in stages)
     vmem = pl.BlockSpec(memory_space=pltpu.VMEM)
     hbm = pl.BlockSpec(memory_space=pltpu.HBM)
     dma = pltpu.SemaphoreType.DMA
@@ -724,6 +822,7 @@
             pltpu.VMEM((2, 1, LANES), f32),
             pltpu.VMEM((n_slots, SUB, LANES), f32),
             dma((PIECES,)),
+            dma((n_edges, PIECES)),
             dma((7,)),
             dma((2, n_edges, PIECES)),
             dma((2, n_edges, PIECES)),
@@ -737,6 +836,9 @@
             dma((2,)),
             dma((n_slots,)),
             dma((n_slots,)),
+            pltpu.SemaphoreType.REGULAR,
+            pltpu.SemaphoreType.REGULAR((max(1, len(stages)),)),
+            pltpu.SemaphoreType.REGULAR((2,)),
         ],
         compiler_params=pltpu.CompilerParams(
             collective_id=0, has_side_effects=True, vmem_limit_bytes=44 * 1024 * 1024

time: 77 us -> 76.5 us (level)
  no operation moved by 1% of the time
where the time goes in v4:
time: 76.5 us; the launch traced here: 76.4 us
  Pallas kernels  76.3 us (100%)
    pallas_call x1, Pallas kernels, local(): pl.pallas_call(functools.partial(kernel, n_pts, n_dir, n_freq), out_shape...  73.6 us
    pallas_call x1, Pallas kernels, local(): pl.pallas_call(functools.partial(finish, n_freq), out_shape=jax.ShapeDtyp...  2.72 us

profile of v4, /device:TPU:0, one launch (start us, length us, event | category | flops | bytes accessed | tf_op | source)
XLA Modules:
  0.0 76.4 jit_solution(17905142797068655541)
XLA Ops:
  0.0 73.6 %shard_map.82 = (f32[24,16,4096]{2,1,0:T(8,128)S(1)}, f32[24,16,256]{2,1,0:T(8,128)S(1)}, f32[24,8,256]{2,1,0:T(8,128)S(1)}, f32[32,16,256]{2,1,0:T(8,128)S(1)},...) custom-call(f32[24,16,4096]{2,1,0:T(8,128)} %action_ref.1, ...), custom_call_target="tpu_custom_call" | custom-call | tf_op jit(solution)/shard_map/pallas_call | solution.py:800
  73.6 2.7 %shard_map.83 = f32[24,16,4096]{2,1,0:T(8,128)} custom-call(f32[24,16,4096]{2,1,0:T(8,128)S(1)} %get-tuple-element.14.done, f32[24,16,256]{2,1,0:T(8,128)S(1)} %get-tuple-element.15.tail_own, f32[24,8,256]{2,1,0:T(8,128)S(1)} %get-tuple-element.16.tail_halo, f32[32,16,256]{2,1,0:T(8,128)S(1)} %get-tuple-element.17.tail_ext, ...), custom_call_target="tpu_custom_call" | custom-call | tf_op jit(solution)/shard_map/pallas_call | solution.py:861

commit v5 on v4

--- a/solution.py
+++ b/solution.py
@@ -16,7 +16,7 @@
 LANES = 128
 HALO = KMAX
 SUB = 8
-PIECES = 4
+PIECES = 2
 LEAD = 1
 
 EPSILON = 1e-06
@@ -440,7 +440,7 @@
             start_edges(1, i, i + 1)
             if i + 1 < PIECES:
                 start_edges(0, i + 1, i + 2)
-        start_inner(1, LEAD)
+        start_inner(1, 3)
 
     @pl.when(dir_at == last_dir)
     def _():

time: 76.5 us -> 76.5 us (level)
  no operation moved by 1% of the time
where the time goes in v5:
time: 76.5 us; the launch traced here: 76.3 us
  Pallas kernels  76.3 us (100%)
    pallas_call x1, Pallas kernels, local(): pl.pallas_call(functools.partial(kernel, n_pts, n_dir, n_freq), out_shape...  73.6 us
    pallas_call x1, Pallas kernels, local(): pl.pallas_call(functools.partial(finish, n_freq), out_shape=jax.ShapeDtyp...  2.72 us

profile of v5, /device:TPU:0, one launch (start us, length us, event | category | flops | bytes accessed | tf_op | source)
XLA Modules:
  0.0 76.3 jit_solution(17096386254233594346)
XLA Ops:
  0.0 73.6 %shard_map.82 = (f32[24,16,4096]{2,1,0:T(8,128)S(1)}, f32[24,16,256]{2,1,0:T(8,128)S(1)}, f32[24,8,256]{2,1,0:T(8,128)S(1)}, f32[32,16,256]{2,1,0:T(8,128)S(1)},...) custom-call(f32[24,16,4096]{2,1,0:T(8,128)} %action_ref.1, ...), custom_call_target="tpu_custom_call" | custom-call | tf_op jit(solution)/shard_map/pallas_call | solution.py:800
  73.6 2.7 %shard_map.83 = f32[24,16,4096]{2,1,0:T(8,128)} custom-call(f32[24,16,4096]{2,1,0:T(8,128)S(1)} %get-tuple-element.14.done, f32[24,16,256]{2,1,0:T(8,128)S(1)} %get-tuple-element.15.tail_own, f32[24,8,256]{2,1,0:T(8,128)S(1)} %get-tuple-element.16.tail_halo, f32[32,16,256]{2,1,0:T(8,128)S(1)} %get-tuple-element.17.tail_ext, ...), custom_call_target="tpu_custom_call" | custom-call | tf_op jit(solution)/shard_map/pallas_call | solution.py:861

commit v6 on v5

--- a/solution.py
+++ b/solution.py
@@ -188,6 +188,35 @@
             return {axis: at + amount * (1 - 2 * lax.rem(lax.div(at, amount), 2))}
         return {axis: lax.rem(at + amount, count)}
 
+    if n_freq == 1:
+        edges = []
+        inner, inner_size = 0, freq_local
+    elif n_freq == 2:
+        edges = [jnp.where(has_above, freq_local - HALO, 0)]
+        inner, inner_size = jnp.where(has_above, 0, HALO), freq_local - HALO
+    else:
+        edges = [0, freq_local - HALO]
+        inner, inner_size = HALO, freq_local - 2 * HALO
+
+    def span(c):
+        return pl.ds(pl.multiple_of(c * CHUNK, CHUNK), CHUNK)
+
+    def piece_span(i):
+        return pl.ds(pl.multiple_of(i * piece, piece), piece)
+
+    def own_part(freqs, i, sem):
+        at = piece_span(i)
+        return pltpu.make_async_copy(action_ref.at[freqs, :, at], own.at[freqs, :, at], sem)
+
+    def own_edge(e, i):
+        return own_part(pl.ds(edges[e], HALO), i, own_edge_sem.at[e, i])
+
+    def own_inner(i):
+        return own_part(pl.ds(inner, inner_size), i, own_sem.at[i])
+
+    for i in range(PIECES):
+        for e in range(len(edges)):
+            own_edge(e, i).start()
     def bit(axis, amount):
         return lax.rem(lax.div(places[axis][0], amount), 2)
 
@@ -226,35 +255,6 @@
         pl.when(up_there)(functools.partial(greet, {axis: places[axis][0] + 1}))
         parents += jnp.minimum(places[axis][0], 1)
 
-    if n_freq == 1:
-        edges = []
-        inner, inner_size = 0, freq_local
-    elif n_freq == 2:
-        edges = [jnp.where(has_above, freq_local - HALO, 0)]
-        inner, inner_size = jnp.where(has_above, 0, HALO), freq_local - HALO
-    else:
-        edges = [0, freq_local - HALO]
-        inner, inner_size = HALO, freq_local - 2 * HALO
-
-    def span(c):
-        return pl.ds(pl.multiple_of(c * CHUNK, CHUNK), CHUNK)
-
-    def piece_span(i):
-        return pl.ds(pl.multiple_of(i * piece, piece), piece)
-
-    def own_part(freqs, i, sem):
-        at = piece_span(i)
-        return pltpu.make_async_copy(action_ref.at[freqs, :, at], own.at[freqs, :, at], sem)
-
-    def own_edge(e, i):
-        return own_part(pl.ds(edges[e], HALO), i, own_edge_sem.at[e, i])
-
-    def own_inner(i):
-        return own_part(pl.ds(inner, inner_size), i, own_sem.at[i])
-
-    for i in range(PIECES):
-        for e in range(len(edges)):
-            own_edge(e, i).start()
     for i in range(PIECES):
         own_inner(i).start()
 

time: 76.5 us -> 76.4 us (level)
  no operation moved by 1% of the time
where the time goes in v6:
time: 76.4 us; the launch traced here: 76.2 us
  Pallas kernels  76.2 us (100%)
    pallas_call x1, Pallas kernels, local(): pl.pallas_call(functools.partial(kernel, n_pts, n_dir, n_freq), out_shape...  73.5 us
    pallas_call x1, Pallas kernels, local(): pl.pallas_call(functools.partial(finish, n_freq), out_shape=jax.ShapeDtyp...  2.72 us

profile of v6, /device:TPU:0, one launch (start us, length us, event | category | flops | bytes accessed | tf_op | source)
XLA Modules:
  0.0 76.2 jit_solution(7455868179567831606)
XLA Ops:
  0.0 73.5 %shard_map.82 = (f32[24,16,4096]{2,1,0:T(8,128)S(1)}, f32[24,16,256]{2,1,0:T(8,128)S(1)}, f32[24,8,256]{2,1,0:T(8,128)S(1)}, f32[32,16,256]{2,1,0:T(8,128)S(1)},...) custom-call(f32[24,16,4096]{2,1,0:T(8,128)} %action_ref.1, ...), custom_call_target="tpu_custom_call" | custom-call | tf_op jit(solution)/shard_map/pallas_call | solution.py:800
  73.5 2.7 %shard_map.83 = f32[24,16,4096]{2,1,0:T(8,128)} custom-call(f32[24,16,4096]{2,1,0:T(8,128)S(1)} %get-tuple-element.14.done, f32[24,16,256]{2,1,0:T(8,128)S(1)} %get-tuple-element.15.tail_own, f32[24,8,256]{2,1,0:T(8,128)S(1)} %get-tuple-element.16.tail_halo, f32[32,16,256]{2,1,0:T(8,128)S(1)} %get-tuple-element.17.tail_ext, ...), custom_call_target="tpu_custom_call" | custom-call | tf_op jit(solution)/shard_map/pallas_call | solution.py:861
